TPU v7x, 32 devices: a whole 2x2x4 slice. The times are simulated.
32 devices in a mesh: cuts: 2 (over x), ma: 8 (over z, y), mb: 2 (over core).
Axes of the slice: x: 2, y: 2, z: 4, core: 2. Of those that a mesh axis runs over, the one named last changes fastest.
Arguments:
- stem_field: bfloat16 [64, 512, 2, 512], P(('cuts', 'ma', 'mb')), parts along dimension 0, may hold values from -6 to 6
- first_branch_tensors: bfloat16 [2, 2, 512, 512], P(None, None, 'ma'), may hold values from -0.1875 to 0.1875
- second_branch_tensors: bfloat16 [2, 2, 512, 512], P(None, None, 'ma'), may hold values from -0.1875 to 0.1875
- relabel: int32 [2, 512], replicated, may hold values from 0 to 511, each once within a row
- sample_block: int32 [8192, 1], P(('cuts', 'ma', 'mb')), parts along dimension 0, may hold values from 0 to 31; in each aligned block of 256 rows (0 to 255, 256 to 511, ...) at most 16 rows name the same one
- sample_state: bfloat16 [8192, 2, 512], P(('cuts', 'ma', 'mb')), parts along dimension 0, may hold values from -0.1875 to 0.1875
Outputs:
- amplitudes: bfloat16 [8192, 2, 512], P(('cuts', 'ma', 'mb')), parts along dimension 0
There are 2 independent parts, one for each index of `cuts`. A program takes and returns all parts, laid end to end along the dimension named above; an argument that names none is the same for every part. Nothing has to cross between parts.
Inputs may be any that keep to these rules, and one draw needn't show every extreme that they name: `relabel`: each row is a permutation of 0 to 511. `sample_block`: within the 256 rows of one device no prefix block is named more than 16 times.
All inputs are finite; a program needn't handle non-finite values.
Results may differ from a plain program's by a relative error of at most 0.0075.
Values may be sent and summed in bfloat16 or wider, within the bound.
No kernel may reach another device: no remote copies, remote signals or barrier semaphores. Data moves between devices by JAX's collectives and lax.ppermute only.
A program may use at most 64 MiB of HBM per device.

v0:
```python
import jax
import jax.numpy as jnp
from jax import lax
from jax.sharding import PartitionSpec as P


def complex_table(matrix):
    real_part = matrix[0]
    imag_part = matrix[1]
    upper_rows = jnp.stack([real_part, imag_part], axis=1)
    lower_rows = jnp.stack([-imag_part, real_part], axis=1)
    return jnp.stack([upper_rows, lower_rows], axis=0)


def regroup(stem_field):
    blocks, row_count, part_count, col_count = stem_field.shape
    first_count = lax.axis_size("ma")
    second_count = lax.axis_size("mb")
    groups = first_count * second_count
    pieces = stem_field.reshape(blocks, groups, row_count // groups, part_count, col_count)
    swapped_modes = lax.all_to_all(pieces, ("ma", "mb"), split_axis=1, concat_axis=1, tiled=True)
    return swapped_modes.reshape(blocks, row_count, part_count, col_count)


def on_device(
    stem_field, first_branch_tensors, second_branch_tensors, relabel, sample_block, sample_state
):
    rounds = first_branch_tensors.shape[0]
    width_first = first_branch_tensors.shape[3]
    every_first, every_second = (
        lax.all_gather(first_branch_tensors, "ma", axis=2, tiled=True),
        lax.all_gather(second_branch_tensors, "ma", axis=2, tiled=True),
    )
    positions = jnp.arange(width_first, dtype=jnp.int32)
    for regroup_round_index in range(rounds):
        stem_field = regroup(stem_field)
        first_matrix = every_first[regroup_round_index]
        second_matrix = every_second[regroup_round_index]
        selector = (relabel[regroup_round_index][:, None] == positions[None, :]).astype(
            jnp.bfloat16
        )
        permuted = jnp.einsum(
            "ij,pio->pjo", selector, first_matrix, preferred_element_type=jnp.float32
        ).astype(jnp.bfloat16)
        stem_field = jnp.einsum(
            "sapb,paqo->soqb",
            stem_field,
            complex_table(permuted),
            preferred_element_type=jnp.float32,
        ).astype(jnp.bfloat16)
        stem_field = jnp.einsum(
            "sapb,pbqo->saqo",
            stem_field,
            complex_table(second_matrix),
            preferred_element_type=jnp.float32,
        ).astype(jnp.bfloat16)
    local_blocks = stem_field.shape[0]
    groups = lax.axis_size("ma") * lax.axis_size("mb")
    block_count = local_blocks * groups
    samples = sample_state.shape[0]
    slot_bound = max(2, 2 * samples // block_count)
    state_width = sample_state.shape[2]
    owner_block = sample_block[:, 0]
    block_hot = (owner_block[:, None] == jnp.arange(block_count, dtype=jnp.int32)[None, :]).astype(
        jnp.bfloat16
    )
    order_index = jnp.arange(samples, dtype=jnp.int32)
    earlier_mask = (order_index[:, None] > order_index[None, :]).astype(jnp.bfloat16)
    earlier = jnp.dot(earlier_mask, block_hot, preferred_element_type=jnp.float32)
    slot_index = jnp.sum(earlier * block_hot.astype(jnp.float32), axis=1)
    slot_hot = (slot_index[:, None] == jnp.arange(slot_bound, dtype=jnp.float32)[None, :]).astype(
        jnp.bfloat16
    )
    dispatch = (block_hot[:, :, None] * slot_hot[:, None, :]).reshape(
        samples, block_count * slot_bound
    )
    outgoing = jnp.einsum(
        "nk,nc->kc",
        dispatch,
        sample_state.reshape(samples, 2 * state_width),
        preferred_element_type=jnp.float32,
    ).astype(jnp.bfloat16)
    outgoing = outgoing.reshape(groups, local_blocks, slot_bound, 2, state_width)
    block_table = jax.vmap(complex_table)(jnp.transpose(stem_field, (0, 2, 3, 1)))
    result = jnp.einsum(
        "gsmpb,spbqa->gsmqa",
        lax.all_to_all(outgoing, ("ma", "mb"), split_axis=0, concat_axis=0, tiled=True),
        block_table,
        preferred_element_type=jnp.float32,
    ).astype(jnp.bfloat16)
    returned = lax.all_to_all(result, ("ma", "mb"), split_axis=0, concat_axis=0, tiled=True)
    width_out = returned.shape[4]
    gathered_rows = returned.reshape(block_count * slot_bound, 2 * width_out)
    amplitudes = jnp.dot(dispatch, gathered_rows, preferred_element_type=jnp.float32).astype(
        jnp.bfloat16
    )
    return amplitudes.reshape(samples, 2, width_out)


def solution(mesh):
    placed = (
        P(("cuts", "ma", "mb"), None, None, None),
        P(None, None, "ma", None),
        P(None, None, "ma", None),
        P(),
        P(("cuts", "ma", "mb"), None),
        P(("cuts", "ma", "mb"), None, None),
    )
    return jax.shard_map(
        on_device,
        mesh=mesh,
        in_specs=placed,
        out_specs=P(("cuts", "ma", "mb"), None, None),
        check_vma=False,
    )
```

profile of v0, /device:TPU:1, one launch (start us, length us, event | category | flops | bytes accessed | tf_op | source)
XLA Modules:
  0.0 280.3 jit_solution(17453023563885691046)
XLA Ops:
  6.5 0.0 all-gather.3.cloned.1.call-start
  6.5 0.7 all-gather.3.cloned.1.call-update
  7.3 0.0 all-gather.5.cloned.1.call-start
  7.3 0.7 all-gather.5.cloned.1.call-update
  8.0 5.4 %copy.33 = bf16[2,16,32,2,512]{4,3,2,0,1:T(2,128)(2,1)} copy(bf16[2,16,32,2,512]{4,3,2,1,0:T(2,128)(2,1)} %bitcast.189) | data formatting | bytes 4194304 | tf_op jit(solution)/shard_map/reshape | solution.py:20
  13.4 7.5 %all-to-all-start = ((bf16[2,16,32,2,512]{4,3,2,0,1:T(2,128)(2,1)}), bf16[2,16,32,2,512]{4,3,2,0,1:T(2,128)(2,1)S(1)}, u32[]{:S(2)}, u32[]{:S(2)}) async-start(bf16[2,16,32,2,512]{4,3,2,0,1:T(2,128)(2,1)} %copy.33), calls=%async_computation | async-start | bytes 4194304 | tf_op jit(solution)/shard_map/all_to_all | solution.py:21
  20.9 0.0 copy-done.7
  20.9 64.5 %all-gather.3.cloned.1.call-done = bf16[2,2,512,512]{3,2,1,0:T(8,128)(2,1)} async-done(((bf16[2,2,64,512]{3,2,1,0:T(8,128)(2,1)}), bf16[2,2,512,512]{3,2,1,0:T(8,128)(2,1)}) %all-gather.3.cloned.1.call-update) | async-done | bytes 2097168 | tf_op jit(solution)/shard_map/all_gather | solution.py:31
  85.4 1.9 fusion.20
  87.4 0.1 slice_bitcast_fusion.10
  87.4 1.1 maximum_bitcast_fusion.11
  88.6 50.2 %all-gather.5.cloned.1.call-done = bf16[2,2,512,512]{3,2,1,0:T(8,128)(2,1)} async-done(((bf16[2,2,64,512]{3,2,1,0:T(8,128)(2,1)}), bf16[2,2,512,512]{3,2,1,0:T(8,128)(2,1)}) %all-gather.5.cloned.1.call-update) | async-done | bytes 2097168 | tf_op jit(solution)/shard_map/all_gather | solution.py:32
  138.8 2.2 fusion.41
  141.0 0.0 copy-done
  141.0 1.2 slice_bitcast_fusion.8
  142.2 1.5 maximum_bitcast_fusion.13
  143.7 0.0 all-to-all-done
  143.7 1.8 copy.34
  145.5 7.0 %bitcast_convert_fusion.3 = bf16[2,512,2,512]{3,1,2,0:T(8,128)(2,1)S(1)} fusion(bf16[1,512,2,512]{3,1,0,2:T(8,128)(2,1)} %get-tuple-element.24, bf16[1,512,2,512]{3,1,0,2:T(8,128)(2,1)} %get-tuple-element.23, bf16[2,512,2,512,1]{3,1,4,2,0:T(8,128)(2,1)} %bitcast.190, bf16[1,512,2,512]{3,1,2,0:T(8,128)(2,1)} %get-tuple-element.22, ...), kind=kOutput, calls=%fused_computation.6 | convolution fusion | flops 4305453056 | bytes 8388608 | tf_op jit(solution)/shard_map/sapb,pbqo->saqo/dot_general | solution.py:51
  152.5 1.4 copy.37
  153.9 6.2 %all-to-all-start.1 = ((bf16[2,16,32,2,512]{4,2,3,0,1:T(8,128)(2,1)}), bf16[2,16,32,2,512]{4,2,3,0,1:T(8,128)(2,1)S(1)}, u32[]{:S(2)}, u32[]{:S(2)}) async-start(bf16[2,16,32,2,512]{4,2,3,0,1:T(8,128)(2,1)} %copy.37), calls=%async_computation.1 | async-start | bytes 4194304 | tf_op jit(solution)/shard_map/all_to_all | solution.py:21
  160.2 0.1 copy.71
  160.3 0.2 fusion.24
  160.5 0.4 convolution_convert_fusion
  161.0 1.6 reshape.149
  162.6 2.6 copy.42
  165.2 0.7 fusion.19
  165.9 0.8 fusion.39
  166.7 1.0 slice_bitcast_fusion.12
  167.8 34.0 %all-to-all-done.1 = bf16[2,16,32,2,512]{4,2,3,0,1:T(8,128)(2,1)S(1)} async-done(((bf16[2,16,32,2,512]{4,2,3,0,1:T(8,128)(2,1)}), bf16[2,16,32,2,512]{4,2,3,0,1:T(8,128)(2,1)S(1)}, u32[]{:S(2)}, u32[]{:S(2)}) %all-to-all-start.1) | async-done | bytes 2097184 | tf_op jit(solution)/shard_map/all_to_all | solution.py:21
  201.8 10.7 %all-to-all-start.2 = ((bf16[16,2,16,2,512]{4,2,3,1,0:T(8,128)(2,1)}), bf16[16,2,16,2,512]{4,2,3,1,0:T(8,128)(2,1)}, u32[]{:S(2)}, u32[]{:S(2)}) async-start(bf16[16,2,16,2,512]{4,2,3,1,0:T(8,128)(2,1)} %copy.42), calls=%async_computation.2 | async-start | bytes 2097152 | tf_op jit(solution)/shard_map/all_to_all | solution.py:87
  212.4 0.0 copy-start.3
  212.4 3.0 %maximum_bitcast_fusion.9 = (bf16[1,512,2,512]{3,1,2,0:T(8,128)(2,1)}, bf16[1,512,2,512]{3,1,2,0:T(8,128)(2,1)}) fusion(bf16[512,1,512]{2,0,1:T(8,128)(2,1)} %get-tuple-element.15, bf16[512,1,512]{2,0,1:T(8,128)(2,1)} %get-tuple-element.16, bf16[512,1,512]{2,0,1:T(8,128)(2,1)S(1)} %copy-done.1), kind=kLoop, calls=%fused_computation.38 | loop fusion | flops 1048576 | bytes 3670016 | tf_op jit(solution)/shard_map/stack | solution.py:12
  215.4 1.6 maximum_bitcast_fusion.15
  217.0 1.5 copy.38
  218.5 0.1 copy-done.5
  218.6 7.0 %fusion.12 = bf16[2,2,512,512]{2,3,1,0:T(8,128)(2,1)S(1)} fusion(bf16[2,512,2,512,1]{3,1,4,2,0:T(8,128)(2,1)} %bitcast.191, bf16[1,512,2,512]{3,1,2,0:T(8,128)(2,1)} %get-tuple-element.20, bf16[1,512,2,512]{3,1,2,0:T(8,128)(2,1)S(1)} %copy-done.5, bf16[1,512,2,512]{3,1,2,0:T(8,128)(2,1)} %get-tuple-element.26, bf16[1,512,2,512]{3,1,2,0:T(8,128)(2,1)} %get-tuple-element.25), kind=kOutput, calls=%fused_computation.24 | convolution fusion | flops 4302307328 | bytes 8388608 | tf_op jit(solution)/shard_map/sapb,pbqo->saqo/dot_general | solution.py:51
  225.7 0.1 fusion.43
  225.7 0.1 slice_bitcast_fusion
  225.9 1.7 maximum_bitcast_fusion.7
  227.6 8.1 %all-to-all-done.2 = bf16[16,2,16,2,512]{4,2,3,1,0:T(8,128)(2,1)} async-done(((bf16[16,2,16,2,512]{4,2,3,1,0:T(8,128)(2,1)}), bf16[16,2,16,2,512]{4,2,3,1,0:T(8,128)(2,1)}, u32[]{:S(2)}, u32[]{:S(2)}) %all-to-all-start.2) | async-done | bytes 1048608 | tf_op jit(solution)/shard_map/all_to_all | solution.py:87
  235.7 3.1 %fusion.21 = bf16[16,2,16,2,512]{4,2,0,3,1:T(8,128)(2,1)S(1)} fusion(bf16[1,2,512,2,512]{2,4,1,3,0:T(8,128)(2,1)} %get-tuple-element.14, bf16[1,2,512,2,512]{2,4,1,3,0:T(8,128)(2,1)S(1)} %get-tuple-element.13, bf16[16,2,16,2,512]{4,2,3,1,0:T(8,128)(2,1)} %all-to-all-done.2), kind=kOutput, calls=%fused_computation.30 | convolution fusion | flops 1076363264 | bytes 6291456 | tf_op jit(solution)/shard_map/gsmpb,spbqa->gsmqa/dot_general | solution.py:85
  238.8 0.1 copy.45
  238.9 31.5 %all_to_all.20 = bf16[16,2,16,2,512]{4,2,3,1,0:T(8,128)(2,1)S(1)} all-to-all(bf16[16,2,16,2,512]{4,2,3,1,0:T(8,128)(2,1)S(1)} %copy.45), channel_id=1, replica_groups=mesh['cuts'=2,'ma'=8,'mb'=2] {'ma','mb'}, dimensions={0} | all-to-all | bytes 2097152 | tf_op jit(solution)/shard_map/all_to_all | solution.py:91
  270.5 1.1 copy.46
  271.6 0.2 copy.72
  271.8 0.5 convolution_convert_fusion.3
  272.3 1.2 reshape.151
  (21 shorter events, 0.1 us)
Async XLA Ops:
  6.5 78.8 %all-gather.3.cloned.1.call-start = ((), (), s32[]{:S(2)}) async-start(), calls=%async_computation.4 | async-start | bytes 2359296 | tf_op jit(solution)/shard_map/all_gather | solution.py:31
  7.3 131.5 %all-gather.5.cloned.1.call-start = ((), (), s32[]{:S(2)}) async-start(), calls=%async_computation.5 | async-start | bytes 2359296 | tf_op jit(solution)/shard_map/all_gather | solution.py:32
  13.4 7.5 %copy-start.7 = (s32[2,512]{1,0:T(2,128)S(1)}, s32[2,512]{1,0:T(2,128)}, u32[]{:S(2)}) copy-start(s32[2,512]{1,0:T(2,128)} %param.9) | copy-start | bytes 12292
  13.4 130.3 %all-to-all-start = ((bf16[2,16,32,2,512]{4,3,2,0,1:T(2,128)(2,1)}), bf16[2,16,32,2,512]{4,3,2,0,1:T(2,128)(2,1)S(1)}, u32[]{:S(2)}, u32[]{:S(2)}) async-start(bf16[2,16,32,2,512]{4,3,2,0,1:T(2,128)(2,1)} %copy.33), calls=%async_computation | async-start | bytes 4194304 | tf_op jit(solution)/shard_map/all_to_all | solution.py:21
  138.8 2.2 copy-start
  153.9 6.2 %copy-start.6 = (bf16[256,2,512]{2,1,0:T(2,128)(2,1)S(1)}, bf16[256,2,512]{2,1,0:T(2,128)(2,1)}, u32[]{:S(2)}) copy-start(bf16[256,2,512]{2,1,0:T(2,128)(2,1)} %param.11) | copy-start | bytes 1572868
  153.9 6.3 %copy-start.8 = (s32[256,1]{0,1:T(1,128)S(1)}, s32[256,1]{0,1:T(1,128)}, u32[]{:S(2)}) copy-start(s32[256,1]{0,1:T(1,128)} %param.10) | copy-start | bytes 3076
  153.9 47.8 %all-to-all-start.1 = ((bf16[2,16,32,2,512]{4,2,3,0,1:T(8,128)(2,1)}), bf16[2,16,32,2,512]{4,2,3,0,1:T(8,128)(2,1)S(1)}, u32[]{:S(2)}, u32[]{:S(2)}) async-start(bf16[2,16,32,2,512]{4,2,3,0,1:T(8,128)(2,1)} %copy.37), calls=%async_computation.1 | async-start | bytes 4194304 | tf_op jit(solution)/shard_map/all_to_all | solution.py:21
  162.6 2.6 copy-start.9
  167.8 44.7 %copy-start.1 = (bf16[512,1,512]{2,0,1:T(8,128)(2,1)S(1)}, bf16[512,1,512]{2,0,1:T(8,128)(2,1)}, u32[]{:S(2)}) copy-start(bf16[512,1,512]{2,0,1:T(8,128)(2,1)} %fusion.39) | copy-start | bytes 1572868
  201.8 33.9 %all-to-all-start.2 = ((bf16[16,2,16,2,512]{4,2,3,1,0:T(8,128)(2,1)}), bf16[16,2,16,2,512]{4,2,3,1,0:T(8,128)(2,1)}, u32[]{:S(2)}, u32[]{:S(2)}) async-start(bf16[16,2,16,2,512]{4,2,3,1,0:T(8,128)(2,1)} %copy.42), calls=%async_computation.2 | async-start | bytes 2097152 | tf_op jit(solution)/shard_map/all_to_all | solution.py:87
  212.4 3.0 %copy-start.2 = (bf16[512,1,512]{2,0,1:T(8,128)(2,1)S(1)}, bf16[512,1,512]{2,0,1:T(8,128)(2,1)}, u32[]{:S(2)}) copy-start(bf16[512,1,512]{2,0,1:T(8,128)(2,1)} %get-tuple-element.12) | copy-start | bytes 1572868
  212.4 3.0 %copy-start.3 = (bf16[512,1,512]{2,0,1:T(8,128)(2,1)S(1)}, bf16[512,1,512]{2,0,1:T(8,128)(2,1)}, u32[]{:S(2)}) copy-start(bf16[512,1,512]{2,0,1:T(8,128)(2,1)} %get-tuple-element.8) | copy-start | bytes 1572868
  212.4 3.0 %copy-start.4 = (bf16[512,1,512]{2,0,1:T(8,128)(2,1)S(1)}, bf16[512,1,512]{2,0,1:T(8,128)(2,1)}, u32[]{:S(2)}) copy-start(bf16[512,1,512]{2,0,1:T(8,128)(2,1)} %get-tuple-element.9) | copy-start | bytes 1572868
  217.0 1.6 copy-start.5
Sparse Core Ops, SparseCore 0:
  9.5 75.8 all-gather.2
  87.6 51.1 all-gather.4
where the time goes:
time: 281 us; the launch traced here: 280 us
  waiting for transfers between devices  158 us (56%)
  blocking collectives  31.5 us (11%)
  starting transfers between devices  24.4 us (9%)
  matrix products  20.9 us (7%)
  local copies, waits for them, and re-layouts  19.5 us (7%)
  between operations  13.6 us (5%)
  other arithmetic  12.2 us (4%)
    all_gather x1, waiting for transfers between devices, on_device(): lax.all_gather(first_branch_tensors, 'ma', axis=2, tiled=True)  64.5 us
    all_gather x1, waiting for transfers between devices, on_device(): lax.all_gather(second_branch_tensors, 'ma', axis=2, tiled=True)  50.2 us
    all_to_all x2, waiting for transfers between devices, regroup(): lax.all_to_all(pieces, ('ma', 'mb'), split_axis=1, concat_axis=1, tiled=T...  34 us
    all_to_all x1, blocking collectives, on_device(): lax.all_to_all(result, ('ma', 'mb'), split_axis=0, concat_axis=0, tiled=T...  31.5 us
    dot_general x2, matrix products, on_device(): jnp.einsum('sapb,pbqo->saqo', stem_field, complex_table(second_matrix), p...  14 us
    all_to_all x2, starting transfers between devices, regroup(): lax.all_to_all(pieces, ('ma', 'mb'), split_axis=1, concat_axis=1, tiled=T...  13.7 us
    all_to_all x1, starting transfers between devices, on_device(): lax.all_to_all(outgoing, ('ma', 'mb'), split_axis=0, concat_axis=0, tiled...  10.7 us
    another operation x5, other arithmetic, complex_table(): return jnp.stack([upper_rows, lower_rows], axis=0)  8.96 us
  transfers between devices with their start and end apart: 5, of which 4 were waited for; matrix products, arithmetic and copies ran while one was open for 13% of the time, Pallas kernels for 0%

commit v1 on v0

--- a/solution.py
+++ b/solution.py
@@ -2,6 +2,22 @@
 import jax.numpy as jnp
 from jax import lax
 from jax.sharding import PartitionSpec as P
+
+
+def pairwise_exchange(x, axis, split, join):
+    ways, here = (lax.axis_size(axis), lax.axis_index(axis))
+    width = x.shape[split] // ways
+    shape = list(x.shape)
+    shape[split] = width
+    height = shape[join]
+    shape[join] = height * ways
+    full = jnp.zeros(shape, x.dtype)
+    for mask in range(ways):
+        part = lax.dynamic_slice_in_dim(x, (here ^ mask) * width, width, axis=split)
+        if mask:
+            part = lax.ppermute(part, axis, [(d, d ^ mask) for d in range(ways)])
+        full = lax.dynamic_update_slice_in_dim(full, part, (here ^ mask) * height, axis=join)
+    return full
 
 
 def complex_table(matrix):
@@ -18,7 +34,7 @@
     second_count = lax.axis_size("mb")
     groups = first_count * second_count
     pieces = stem_field.reshape(blocks, groups, row_count // groups, part_count, col_count)
-    swapped_modes = lax.all_to_all(pieces, ("ma", "mb"), split_axis=1, concat_axis=1, tiled=True)
+    swapped_modes = pairwise_exchange(pieces, ("ma", "mb"), 1, 1)
     return swapped_modes.reshape(blocks, row_count, part_count, col_count)
 
 

time: 281 us -> 273 us (0.972)
  waiting for transfers between devices: 158 us -> 109 us
  starting transfers between devices: 24.4 us -> 57 us
  blocking collectives: 31.5 us -> 38.9 us
  other arithmetic: 12.2 us -> 8.97 us
    ppermute x0 -> x30, waiting for transfers between devices: none -> 80.9 us  [pairwise_exchange(): part = lax.ppermute(part, axis, [(d, d ^ mask) for d in range(ways)])]
    all_gather x1, waiting for transfers between devices: 64.5 us -> 0.02 us  [on_device(): lax.all_gather(first_branch_tensors, 'ma', axis=2, tiled=True)]
    ppermute x0 -> x30, starting transfers between devices: none -> 50.5 us  [pairwise_exchange(): part = lax.ppermute(part, axis, [(d, d ^ mask) for d in range(ways)])]
    all_to_all x2 -> x0, waiting for transfers between devices: 34 us -> none  [regroup(): lax.all_to_all(pieces, ('ma', 'mb'), split_axis=1, concat_axis=1, tiled=T...]
    all_gather x1, waiting for transfers between devices: 50.2 us -> 26.6 us  [on_device(): lax.all_gather(second_branch_tensors, 'ma', axis=2, tiled=True)]
    all_to_all x2 -> x0, starting transfers between devices: 13.7 us -> none  [regroup(): lax.all_to_all(pieces, ('ma', 'mb'), split_axis=1, concat_axis=1, tiled=T...]
    all_to_all x1, waiting for transfers between devices: 8.1 us -> 0.01 us  [on_device(): lax.all_to_all(outgoing, ('ma', 'mb'), split_axis=0, concat_axis=0, tiled...]
    all_to_all x1, blocking collectives: 31.5 us -> 38.9 us  [on_device(): lax.all_to_all(result, ('ma', 'mb'), split_axis=0, concat_axis=0, tiled=T...]
  transfers between devices with their start and end apart: 5 -> 33, of which waited for: 4 -> 12; matrix products, arithmetic and copies ran while one was open for 13% -> 16% of each run, Pallas kernels for 0% -> 0%
where the time goes in v1:
time: 273 us; the launch traced here: 272 us
  waiting for transfers between devices  109 us (40%)
  starting transfers between devices  57 us (21%)
  blocking collectives  38.9 us (14%)
  matrix products  22.2 us (8%)
  local copies, waits for them, and re-layouts  22.1 us (8%)
  between operations  14.1 us (5%)
  other arithmetic  8.97 us (3%)
    ppermute x30, waiting for transfers between devices, pairwise_exchange(): part = lax.ppermute(part, axis, [(d, d ^ mask) for d in range(ways)])  80.9 us
    ppermute x30, starting transfers between devices, pairwise_exchange(): part = lax.ppermute(part, axis, [(d, d ^ mask) for d in range(ways)])  50.5 us
    all_to_all x1, blocking collectives, on_device(): lax.all_to_all(result, ('ma', 'mb'), split_axis=0, concat_axis=0, tiled=T...  38.9 us
    all_gather x1, waiting for transfers between devices, on_device(): lax.all_gather(second_branch_tensors, 'ma', axis=2, tiled=True)  26.6 us
    dot_general x2, matrix products, on_device(): jnp.einsum('sapb,pbqo->saqo', stem_field, complex_table(second_matrix), p...  15.3 us
    another operation x5, other arithmetic, complex_table(): return jnp.stack([upper_rows, lower_rows], axis=0)  7.92 us
    all_to_all x1, starting transfers between devices, on_device(): lax.all_to_all(outgoing, ('ma', 'mb'), split_axis=0, concat_axis=0, tiled...  6.32 us
  transfers between devices with their start and end apart: 33, of which 12 were waited for; matrix products, arithmetic and copies ran while one was open for 16% of the time, Pallas kernels for 0%

profile of v1, /device:TPU:1, one launch (start us, length us, event | category | flops | bytes accessed | tf_op | source)
XLA Modules:
  0.0 272.1 jit_solution(6590454631538353851)
XLA Ops:
  7.4 4.4 %constant_dynamic-slice_fusion.15 = (bf16[2,1,32,2,512]{4,3,2,1,0:T(2,128)(2,1)S(1)}, bf16[2,1,32,2,512]{4,3,2,1,0:T(2,128)(2,1)S(1)}, bf16[2,1,32,2,512]{4,3,2,...) fusion(bf16[2,16,32,2,512]{4,3,2,1,0:T(2,128)(2,1)} %bitcast.19, ...), kind=kLoop, calls=%fused_computation.112 | loop fusion | bytes 4194368 | tf_op jit(solution)/shard_map/dynamic_slice | solution.py:16
  11.8 2.7 collective-permute-start.1
  14.5 1.7 collective-permute-start.3
  18.1 1.2 copy.72
  19.3 6.3 %all-to-all-start = ((bf16[16,2,16,2,512]{4,2,3,1,0:T(8,128)(2,1)}), bf16[16,2,16,2,512]{4,2,3,1,0:T(8,128)(2,1)}, u32[]{:S(2)}, u32[]{:S(2)}) async-start(bf16[16,2,16,2,512]{4,2,3,1,0:T(8,128)(2,1)} %copy.72), calls=%async_computation | async-start | bytes 2097152 | tf_op jit(solution)/shard_map/all_to_all | solution.py:103
  26.7 2.3 collective-permute-start.5
  31.4 2.6 collective-permute-start.7
  36.2 3.0 %collective-permute-start.9 = (bf16[2,1,32,2,512]{4,3,2,1,0:T(2,128)(2,1)S(1)}, bf16[2,1,32,2,512]{4,3,2,1,0:T(2,128)(2,1)S(1)}, u32[]{:S(2)}, u32[]{:S(2)}) collective-permute-start(bf16[2,1,32,2,512]{4,3,2,1,0:T(2,128)(2,1)S(1)} %get-tuple-element.28), channel_id=1, source_target_pairs={{0,10},{1,11},{2,8},{3,9},{4,14},{5,15},{6,12},{7,13},{8,2},{9,3},... | collective-permute-start | bytes 393224 | tf_op jit(solution)/shard_map/ppermute | solution.py:18
  40.1 14.4 %collective-permute-done.5 = bf16[2,1,32,2,512]{4,3,2,1,0:T(2,128)(2,1)S(1)} collective-permute-done((bf16[2,1,32,2,512]{4,3,2,1,0:T(2,128)(2,1)}, bf16[2,1,32,2,512]{4,3,2,1,0:T(2,128)(2,1)S(1)}, u32[]{:S(2)}, u32[]{:S(2)}) %collective-permute-start.5) | collective-permute-done | bytes 131104 | tf_op jit(solution)/shard_map/ppermute | solution.py:18
  54.6 4.4 %collective-permute-start.10 = (bf16[2,1,32,2,512]{4,3,2,1,0:T(2,128)(2,1)S(1)}, bf16[2,1,32,2,512]{4,3,2,1,0:T(2,128)(2,1)S(1)}, u32[]{:S(2)}, u32[]{:S(2)}) collective-permute-start(bf16[2,1,32,2,512]{4,3,2,1,0:T(2,128)(2,1)S(1)} %get-tuple-element.27), channel_id=1, source_target_pairs={{0,11},{1,10},{2,9},{3,8},{4,15},{5,14},{6,13},{7,12},{8,3},{9,2},... | collective-permute-start | bytes 393224 | tf_op jit(solution)/shard_map/ppermute | solution.py:18
  59.0 4.0 %collective-permute-done.6 = bf16[2,1,32,2,512]{4,3,2,1,0:T(2,128)(2,1)S(1)} collective-permute-done((bf16[2,1,32,2,512]{4,3,2,1,0:T(2,128)(2,1)}, bf16[2,1,32,2,512]{4,3,2,1,0:T(2,128)(2,1)S(1)}, u32[]{:S(2)}, u32[]{:S(2)}) %collective-permute-start.6) | collective-permute-done | bytes 131104 | tf_op jit(solution)/shard_map/ppermute | solution.py:18
  63.0 3.8 %collective-permute-start.11 = (bf16[2,1,32,2,512]{4,3,2,1,0:T(2,128)(2,1)S(1)}, bf16[2,1,32,2,512]{4,3,2,1,0:T(2,128)(2,1)S(1)}, u32[]{:S(2)}, u32[]{:S(2)}) collective-permute-start(bf16[2,1,32,2,512]{4,3,2,1,0:T(2,128)(2,1)S(1)} %get-tuple-element.26), channel_id=1, source_target_pairs={{0,12},{1,13},{2,14},{3,15},{4,8},{5,9},{6,10},{7,11},{8,4},{9,5},... | collective-permute-start | bytes 393224 | tf_op jit(solution)/shard_map/ppermute | solution.py:18
  66.8 22.6 %collective-permute-done.7 = bf16[2,1,32,2,512]{4,3,2,1,0:T(2,128)(2,1)S(1)} collective-permute-done((bf16[2,1,32,2,512]{4,3,2,1,0:T(2,128)(2,1)S(1)}, bf16[2,1,32,2,512]{4,3,2,1,0:T(2,128)(2,1)S(1)}, u32[]{:S(2)}, u32[]{:S(2)}) %collective-permute-start.7) | collective-permute-done | bytes 131104 | tf_op jit(solution)/shard_map/ppermute | solution.py:18
  89.5 1.2 collective-permute-start.12
  90.7 2.2 collective-permute-done.8
  92.9 2.0 collective-permute-start.13
  94.9 7.4 %collective-permute-done.9 = bf16[2,1,32,2,512]{4,3,2,1,0:T(2,128)(2,1)S(1)} collective-permute-done((bf16[2,1,32,2,512]{4,3,2,1,0:T(2,128)(2,1)S(1)}, bf16[2,1,32,2,512]{4,3,2,1,0:T(2,128)(2,1)S(1)}, u32[]{:S(2)}, u32[]{:S(2)}) %collective-permute-start.9) | collective-permute-done | bytes 131104 | tf_op jit(solution)/shard_map/ppermute | solution.py:18
  102.2 1.6 collective-permute-start.14
  103.9 1.2 collective-permute-done.10
  105.2 8.2 %collective-permute-done.14 = bf16[2,1,32,2,512]{4,3,2,1,0:T(2,128)(2,1)S(1)} collective-permute-done((bf16[2,1,32,2,512]{4,3,2,1,0:T(2,128)(2,1)S(1)}, bf16[2,1,32,2,512]{4,3,2,1,0:T(2,128)(2,1)S(1)}, u32[]{:S(2)}, u32[]{:S(2)}) %collective-permute-start.14) | collective-permute-done | bytes 131104 | tf_op jit(solution)/shard_map/ppermute | solution.py:18
  113.4 1.9 fusion.20
  115.5 1.5 maximum_bitcast_fusion.11
  119.5 26.6 %all-gather.5.cloned.1.call-done = bf16[2,2,512,512]{3,2,1,0:T(8,128)(2,1)} async-done(((bf16[2,2,64,512]{3,2,1,0:T(8,128)(2,1)}), bf16[2,2,512,512]{3,2,1,0:T(8,128)(2,1)}) %all-gather.5.cloned.1.call-update) | async-done | bytes 2097168 | tf_op jit(solution)/shard_map/all_gather | solution.py:48
  146.1 2.8 %slice_bitcast_fusion.8 = (bf16[512,1,512]{2,0,1:T(8,128)(2,1)S(1)}, bf16[512,1,512]{2,0,1:T(8,128)(2,1)}, bf16[512,1,512]{2,0,1:T(8,128)(2,1)}, bf16[512,1,512]{2,0,1:T(8,128)(2,1)S(1)}) fusion(bf16[2,2,512,512]{3,2,1,0:T(8,128)(2,1)} %all-gather.5.cloned.1.call-done), kind=kLoop, calls=%fused_computation.53 | loop fusion | bytes 4194304 | tf_op jit(solution)/shard_map/stack;squeeze | solution.py:26
  149.7 1.6 maximum_bitcast_fusion.13
  151.3 8.1 %bitcast_convert_fusion.3 = bf16[2,512,2,512]{3,1,2,0:T(8,128)(2,1)} fusion(bf16[1,512,2,512]{3,1,0,2:T(8,128)(2,1)} %get-tuple-element.56, bf16[1,512,2,512]{3,1,0,2:T(8,128)(2,1)} %get-tuple-element.55, bf16[2,512,2,512,1]{3,1,4,2,0:T(8,128)(2,1)S(1)} %bitcast.190, bf16[1,512,2,512]{3,1,2,0:T(8,128)(2,1)} %get-tuple-element.54, ...), kind=kOutput, calls=%fused_computation.6 | convolution fusion | flops 4305453056 | bytes 8388608 | tf_op jit(solution)/shard_map/sapb,pbqo->saqo/dot_general | solution.py:67
  159.6 1.3 copy-done.2
  162.6 1.4 collective-permute-start.17
  164.0 1.2 collective-permute-start.18
  165.8 1.6 maximum_bitcast_fusion.9
  167.4 1.5 maximum_bitcast_fusion.15
  170.1 1.5 collective-permute-start.21
  171.7 1.6 collective-permute-start.22
  173.3 1.2 collective-permute-start.23
  174.5 1.6 collective-permute-start.24
  176.1 3.4 %collective-permute-start.25 = (bf16[2,1,32,2,512]{4,2,1,3,0:T(8,128)(2,1)S(1)}, bf16[2,1,32,2,512]{4,2,1,3,0:T(8,128)(2,1)S(1)}, u32[]{:S(2)}, u32[]{:S(2)}) collective-permute-start(bf16[2,1,32,2,512]{4,2,1,3,0:T(8,128)(2,1)S(1)} %get-tuple-element.11), channel_id=1, source_target_pairs={{0,11},{1,10},{2,9},{3,8},{4,15},{5,14},{6,13},{7,12},{8,3},{9,2},... | collective-permute-start | bytes 393224 | tf_op jit(solution)/shard_map/ppermute | solution.py:18
  179.5 2.8 %collective-permute-done.21 = bf16[2,1,32,2,512]{4,2,1,3,0:T(8,128)(2,1)S(1)} collective-permute-done((bf16[2,1,32,2,512]{4,2,1,3,0:T(8,128)(2,1)S(1)}, bf16[2,1,32,2,512]{4,2,1,3,0:T(8,128)(2,1)S(1)}, u32[]{:S(2)}, u32[]{:S(2)}) %collective-permute-start.21) | collective-permute-done | bytes 131104 | tf_op jit(solution)/shard_map/ppermute | solution.py:18
  182.3 1.7 collective-permute-start.26
  184.0 1.6 collective-permute-start.27
  185.7 12.8 %collective-permute-done.23 = bf16[2,1,32,2,512]{4,2,1,3,0:T(8,128)(2,1)S(1)} collective-permute-done((bf16[2,1,32,2,512]{4,2,1,3,0:T(8,128)(2,1)S(1)}, bf16[2,1,32,2,512]{4,2,1,3,0:T(8,128)(2,1)S(1)}, u32[]{:S(2)}, u32[]{:S(2)}) %collective-permute-start.23) | collective-permute-done | bytes 131104 | tf_op jit(solution)/shard_map/ppermute | solution.py:18
  198.4 1.4 collective-permute-start.28
  200.0 4.1 %collective-permute-start.29 = (bf16[2,1,32,2,512]{4,2,1,3,0:T(8,128)(2,1)S(1)}, bf16[2,1,32,2,512]{4,2,1,3,0:T(8,128)(2,1)S(1)}, u32[]{:S(2)}, u32[]{:S(2)}) collective-permute-start(bf16[2,1,32,2,512]{4,2,1,3,0:T(8,128)(2,1)S(1)} %get-tuple-element.7), channel_id=1, source_target_pairs={{0,15},{1,14},{2,13},{3,12},{4,11},{5,10},{6,9},{7,8},{8,7},{9,6},... | collective-permute-start | bytes 393224 | tf_op jit(solution)/shard_map/ppermute | solution.py:18
  204.2 5.2 %collective-permute-done.25 = bf16[2,1,32,2,512]{4,2,1,3,0:T(8,128)(2,1)S(1)} collective-permute-done((bf16[2,1,32,2,512]{4,2,1,3,0:T(8,128)(2,1)S(1)}, bf16[2,1,32,2,512]{4,2,1,3,0:T(8,128)(2,1)S(1)}, u32[]{:S(2)}, u32[]{:S(2)}) %collective-permute-start.25) | collective-permute-done | bytes 131104 | tf_op jit(solution)/shard_map/ppermute | solution.py:18
  209.5 1.3 copy-done.1
  210.9 7.2 %fusion.12 = bf16[2,2,512,512]{2,3,1,0:T(8,128)(2,1)S(1)} fusion(bf16[2,512,2,512,1]{3,1,4,2,0:T(8,128)(2,1)} %bitcast.189, bf16[1,512,2,512]{3,1,2,0:T(8,128)(2,1)} %get-tuple-element.52, bf16[1,512,2,512]{3,1,2,0:T(8,128)(2,1)S(1)} %copy-done.7, bf16[1,512,2,512]{3,1,2,0:T(8,128)(2,1)} %get-tuple-element.58, bf16[1,512,2,512]{3,1,2,0:T(8,128)(2,1)} %get-tuple-element.57), kind=kOutput, calls=%fused_computation.24 | convolution fusion | flops 4302307328 | bytes 8388608 | tf_op jit(solution)/shard_map/sapb,pbqo->saqo/dot_general | solution.py:67
  218.3 1.7 maximum_bitcast_fusion.7
  220.1 3.1 %fusion.21 = bf16[16,2,16,2,512]{4,2,0,3,1:T(8,128)(2,1)S(1)} fusion(bf16[1,2,512,2,512]{2,4,1,3,0:T(8,128)(2,1)} %get-tuple-element.46, bf16[1,2,512,2,512]{2,4,1,3,0:T(8,128)(2,1)S(1)} %get-tuple-element.45, bf16[16,2,16,2,512]{4,2,3,1,0:T(8,128)(2,1)} %all-to-all-done), kind=kOutput, calls=%fused_computation.30 | convolution fusion | flops 1076363264 | bytes 6291456 | tf_op jit(solution)/shard_map/gsmpb,spbqa->gsmqa/dot_general | solution.py:101
  223.3 38.9 %all_to_all.10 = bf16[16,2,16,2,512]{4,2,3,1,0:T(8,128)(2,1)S(1)} all-to-all(bf16[16,2,16,2,512]{4,2,3,1,0:T(8,128)(2,1)S(1)} %copy.75), channel_id=1, replica_groups=mesh['cuts'=2,'ma'=8,'mb'=2] {'ma','mb'}, dimensions={0} | all-to-all | bytes 2097152 | tf_op jit(solution)/shard_map/all_to_all | solution.py:107
  (112 shorter events, 19.9 us)
Async XLA Ops:
  6.5 106.9 %all-gather.3.cloned.1.call-start = ((), (), s32[]{:S(2)}) async-start(), calls=%async_computation.2 | async-start | bytes 2359296 | tf_op jit(solution)/shard_map/all_gather | solution.py:47
  7.3 9.2 %copy-start.8 = (bf16[256,2,512]{2,1,0:T(2,128)(2,1)S(1)}, bf16[256,2,512]{2,1,0:T(2,128)(2,1)}, u32[]{:S(2)}) copy-start(bf16[256,2,512]{2,1,0:T(2,128)(2,1)} %param.11) | copy-start | bytes 1572868
  7.4 9.2 %copy-start.10 = (s32[256,1]{0,1:T(1,128)S(1)}, s32[256,1]{0,1:T(1,128)}, u32[]{:S(2)}) copy-start(s32[256,1]{0,1:T(1,128)} %param.10) | copy-start | bytes 3076
  11.7 15.0 %collective-permute-start = (bf16[2,1,32,2,512]{4,3,2,1,0:T(2,128)(2,1)}, bf16[2,1,32,2,512]{4,3,2,1,0:T(2,128)(2,1)}, u32[]{:S(2)}, u32[]{:S(2)}) collective-permute-start(bf16[2,1,32,2,512]{4,3,2,1,0:T(2,128)(2,1)} %get-tuple-element.37), channel_id=1, source_target_pairs={{0,1},{1,0},{2,3},{3,2},{4,5},{5,4},{6,7},{7,6},{8,9},{9,8},{10,11... | collective-permute-start | bytes 393224 | tf_op jit(solution)/shard_map/ppermute | solution.py:18
  11.8 18.2 %collective-permute-start.1 = (bf16[2,1,32,2,512]{4,3,2,1,0:T(2,128)(2,1)}, bf16[2,1,32,2,512]{4,3,2,1,0:T(2,128)(2,1)}, u32[]{:S(2)}, u32[]{:S(2)}) collective-permute-start(bf16[2,1,32,2,512]{4,3,2,1,0:T(2,128)(2,1)} %get-tuple-element.36), channel_id=1, source_target_pairs={{0,2},{1,3},{2,0},{3,1},{4,6},{5,7},{6,4},{7,5},{8,10},{9,11},{10,... | collective-permute-start | bytes 393224 | tf_op jit(solution)/shard_map/ppermute | solution.py:18
  14.5 16.9 %collective-permute-start.2 = (bf16[2,1,32,2,512]{4,3,2,1,0:T(2,128)(2,1)}, bf16[2,1,32,2,512]{4,3,2,1,0:T(2,128)(2,1)}, u32[]{:S(2)}, u32[]{:S(2)}) collective-permute-start(bf16[2,1,32,2,512]{4,3,2,1,0:T(2,128)(2,1)} %get-tuple-element.35), channel_id=1, source_target_pairs={{0,3},{1,2},{2,1},{3,0},{4,7},{5,6},{6,5},{7,4},{8,11},{9,10},{10,... | collective-permute-start | bytes 393224 | tf_op jit(solution)/shard_map/ppermute | solution.py:18
  14.5 20.4 %collective-permute-start.3 = (bf16[2,1,32,2,512]{4,3,2,1,0:T(2,128)(2,1)}, bf16[2,1,32,2,512]{4,3,2,1,0:T(2,128)(2,1)}, u32[]{:S(2)}, u32[]{:S(2)}) collective-permute-start(bf16[2,1,32,2,512]{4,3,2,1,0:T(2,128)(2,1)} %get-tuple-element.34), channel_id=1, source_target_pairs={{0,4},{1,5},{2,6},{3,7},{4,0},{5,1},{6,2},{7,3},{8,12},{9,13},{10,... | collective-permute-start | bytes 393224 | tf_op jit(solution)/shard_map/ppermute | solution.py:18
  16.2 20.0 %collective-permute-start.4 = (bf16[2,1,32,2,512]{4,3,2,1,0:T(2,128)(2,1)}, bf16[2,1,32,2,512]{4,3,2,1,0:T(2,128)(2,1)}, u32[]{:S(2)}, u32[]{:S(2)}) collective-permute-start(bf16[2,1,32,2,512]{4,3,2,1,0:T(2,128)(2,1)} %get-tuple-element.33), channel_id=1, source_target_pairs={{0,5},{1,4},{2,7},{3,6},{4,1},{5,0},{6,3},{7,2},{8,13},{9,12},{10,... | collective-permute-start | bytes 393224 | tf_op jit(solution)/shard_map/ppermute | solution.py:18
  19.3 7.3 %copy-start.9 = (s32[2,512]{1,0:T(2,128)S(1)}, s32[2,512]{1,0:T(2,128)}, u32[]{:S(2)}) copy-start(s32[2,512]{1,0:T(2,128)} %param.9) | copy-start | bytes 12292
  19.3 200.7 %all-to-all-start = ((bf16[16,2,16,2,512]{4,2,3,1,0:T(8,128)(2,1)}), bf16[16,2,16,2,512]{4,2,3,1,0:T(8,128)(2,1)}, u32[]{:S(2)}, u32[]{:S(2)}) async-start(bf16[16,2,16,2,512]{4,2,3,1,0:T(8,128)(2,1)} %copy.72), calls=%async_computation | async-start | bytes 2097152 | tf_op jit(solution)/shard_map/all_to_all | solution.py:103
  25.7 120.4 %all-gather.5.cloned.1.call-start = ((), (), s32[]{:S(2)}) async-start(), calls=%async_computation.3 | async-start | bytes 2359296 | tf_op jit(solution)/shard_map/all_gather | solution.py:48
  26.7 27.8 %collective-permute-start.5 = (bf16[2,1,32,2,512]{4,3,2,1,0:T(2,128)(2,1)}, bf16[2,1,32,2,512]{4,3,2,1,0:T(2,128)(2,1)S(1)}, u32[]{:S(2)}, u32[]{:S(2)}) collective-permute-start(bf16[2,1,32,2,512]{4,3,2,1,0:T(2,128)(2,1)} %get-tuple-element.32), channel_id=1, source_target_pairs={{0,6},{1,7},{2,4},{3,5},{4,2},{5,3},{6,0},{7,1},{8,14},{9,15},{10,... | collective-permute-start | bytes 393224 | tf_op jit(solution)/shard_map/ppermute | solution.py:18
  30.0 33.1 %collective-permute-start.6 = (bf16[2,1,32,2,512]{4,3,2,1,0:T(2,128)(2,1)}, bf16[2,1,32,2,512]{4,3,2,1,0:T(2,128)(2,1)S(1)}, u32[]{:S(2)}, u32[]{:S(2)}) collective-permute-start(bf16[2,1,32,2,512]{4,3,2,1,0:T(2,128)(2,1)} %get-tuple-element.31), channel_id=1, source_target_pairs={{0,7},{1,6},{2,5},{3,4},{4,3},{5,2},{6,1},{7,0},{8,15},{9,14},{10,... | collective-permute-start | bytes 393224 | tf_op jit(solution)/shard_map/ppermute | solution.py:18
  31.4 58.1 %collective-permute-start.7 = (bf16[2,1,32,2,512]{4,3,2,1,0:T(2,128)(2,1)S(1)}, bf16[2,1,32,2,512]{4,3,2,1,0:T(2,128)(2,1)S(1)}, u32[]{:S(2)}, u32[]{:S(2)}) collective-permute-start(bf16[2,1,32,2,512]{4,3,2,1,0:T(2,128)(2,1)S(1)} %get-tuple-element.30), channel_id=1, source_target_pairs={{0,8},{1,9},{2,10},{3,11},{4,12},{5,13},{6,14},{7,15},{8,0},{9,1},... | collective-permute-start | bytes 393224 | tf_op jit(solution)/shard_map/ppermute | solution.py:18
  34.9 58.0 %collective-permute-start.8 = (bf16[2,1,32,2,512]{4,3,2,1,0:T(2,128)(2,1)S(1)}, bf16[2,1,32,2,512]{4,3,2,1,0:T(2,128)(2,1)S(1)}, u32[]{:S(2)}, u32[]{:S(2)}) collective-permute-start(bf16[2,1,32,2,512]{4,3,2,1,0:T(2,128)(2,1)S(1)} %get-tuple-element.29), channel_id=1, source_target_pairs={{0,9},{1,8},{2,11},{3,10},{4,13},{5,12},{6,15},{7,14},{8,1},{9,0},... | collective-permute-start | bytes 393224 | tf_op jit(solution)/shard_map/ppermute | solution.py:18
  36.2 66.0 %collective-permute-start.9 = (bf16[2,1,32,2,512]{4,3,2,1,0:T(2,128)(2,1)S(1)}, bf16[2,1,32,2,512]{4,3,2,1,0:T(2,128)(2,1)S(1)}, u32[]{:S(2)}, u32[]{:S(2)}) collective-permute-start(bf16[2,1,32,2,512]{4,3,2,1,0:T(2,128)(2,1)S(1)} %get-tuple-element.28), channel_id=1, source_target_pairs={{0,10},{1,11},{2,8},{3,9},{4,14},{5,15},{6,12},{7,13},{8,2},{9,3},... | collective-permute-start | bytes 393224 | tf_op jit(solution)/shard_map/ppermute | solution.py:18
  54.6 50.5 %collective-permute-start.10 = (bf16[2,1,32,2,512]{4,3,2,1,0:T(2,128)(2,1)S(1)}, bf16[2,1,32,2,512]{4,3,2,1,0:T(2,128)(2,1)S(1)}, u32[]{:S(2)}, u32[]{:S(2)}) collective-permute-start(bf16[2,1,32,2,512]{4,3,2,1,0:T(2,128)(2,1)S(1)} %get-tuple-element.27), channel_id=1, source_target_pairs={{0,11},{1,10},{2,9},{3,8},{4,15},{5,14},{6,13},{7,12},{8,3},{9,2},... | collective-permute-start | bytes 393224 | tf_op jit(solution)/shard_map/ppermute | solution.py:18
  63.0 42.0 %collective-permute-start.11 = (bf16[2,1,32,2,512]{4,3,2,1,0:T(2,128)(2,1)S(1)}, bf16[2,1,32,2,512]{4,3,2,1,0:T(2,128)(2,1)S(1)}, u32[]{:S(2)}, u32[]{:S(2)}) collective-permute-start(bf16[2,1,32,2,512]{4,3,2,1,0:T(2,128)(2,1)S(1)} %get-tuple-element.26), channel_id=1, source_target_pairs={{0,12},{1,13},{2,14},{3,15},{4,8},{5,9},{6,10},{7,11},{8,4},{9,5},... | collective-permute-start | bytes 393224 | tf_op jit(solution)/shard_map/ppermute | solution.py:18
  89.5 15.6 %collective-permute-start.12 = (bf16[2,1,32,2,512]{4,3,2,1,0:T(2,128)(2,1)S(1)}, bf16[2,1,32,2,512]{4,3,2,1,0:T(2,128)(2,1)S(1)}, u32[]{:S(2)}, u32[]{:S(2)}) collective-permute-start(bf16[2,1,32,2,512]{4,3,2,1,0:T(2,128)(2,1)S(1)} %get-tuple-element.25), channel_id=1, source_target_pairs={{0,13},{1,12},{2,15},{3,14},{4,9},{5,8},{6,11},{7,10},{8,5},{9,4},... | collective-permute-start | bytes 393224 | tf_op jit(solution)/shard_map/ppermute | solution.py:18
  92.9 12.2 %collective-permute-start.13 = (bf16[2,1,32,2,512]{4,3,2,1,0:T(2,128)(2,1)S(1)}, bf16[2,1,32,2,512]{4,3,2,1,0:T(2,128)(2,1)S(1)}, u32[]{:S(2)}, u32[]{:S(2)}) collective-permute-start(bf16[2,1,32,2,512]{4,3,2,1,0:T(2,128)(2,1)S(1)} %get-tuple-element.24), channel_id=1, source_target_pairs={{0,14},{1,15},{2,12},{3,13},{4,10},{5,11},{6,8},{7,9},{8,6},{9,7},... | collective-permute-start | bytes 393224 | tf_op jit(solution)/shard_map/ppermute | solution.py:18
  102.2 11.2 %collective-permute-start.14 = (bf16[2,1,32,2,512]{4,3,2,1,0:T(2,128)(2,1)S(1)}, bf16[2,1,32,2,512]{4,3,2,1,0:T(2,128)(2,1)S(1)}, u32[]{:S(2)}, u32[]{:S(2)}) collective-permute-start(bf16[2,1,32,2,512]{4,3,2,1,0:T(2,128)(2,1)S(1)} %get-tuple-element.23), channel_id=1, source_target_pairs={{0,15},{1,14},{2,13},{3,12},{4,11},{5,10},{6,9},{7,8},{8,7},{9,6},... | collective-permute-start | bytes 393224 | tf_op jit(solution)/shard_map/ppermute | solution.py:18
  115.5 2.4 copy-start.11
  146.1 2.8 %copy-start = (bf16[2,2,512,512]{3,2,1,0:T(8,128)(2,1)S(1)}, bf16[2,2,512,512]{3,2,1,0:T(8,128)(2,1)}, u32[]{:S(2)}) copy-start(bf16[2,2,512,512]{3,2,1,0:T(8,128)(2,1)} %all-gather.5.cloned.1.call-done) | copy-start | bytes 6291460
  159.3 1.6 copy-start.2
  160.9 4.9 %copy-start.3 = (bf16[512,1,512]{2,0,1:T(8,128)(2,1)S(1)}, bf16[512,1,512]{2,0,1:T(8,128)(2,1)}, u32[]{:S(2)}) copy-start(bf16[512,1,512]{2,0,1:T(8,128)(2,1)} %get-tuple-element.48) | copy-start | bytes 1572868
  161.2 6.2 %copy-start.4 = (bf16[512,1,512]{2,0,1:T(8,128)(2,1)S(1)}, bf16[512,1,512]{2,0,1:T(8,128)(2,1)}, u32[]{:S(2)}) copy-start(bf16[512,1,512]{2,0,1:T(8,128)(2,1)} %get-tuple-element.44) | copy-start | bytes 1572868
  161.2 6.2 %copy-start.5 = (bf16[512,1,512]{2,0,1:T(8,128)(2,1)S(1)}, bf16[512,1,512]{2,0,1:T(8,128)(2,1)}, u32[]{:S(2)}) copy-start(bf16[512,1,512]{2,0,1:T(8,128)(2,1)} %get-tuple-element.40) | copy-start | bytes 1572868
  161.2 6.2 %copy-start.6 = (bf16[512,1,512]{2,0,1:T(8,128)(2,1)S(1)}, bf16[512,1,512]{2,0,1:T(8,128)(2,1)}, u32[]{:S(2)}) copy-start(bf16[512,1,512]{2,0,1:T(8,128)(2,1)} %get-tuple-element.41) | copy-start | bytes 1572868
  161.2 7.7 %collective-permute-start.15 = (bf16[2,1,32,2,512]{4,2,1,3,0:T(8,128)(2,1)S(1)}, bf16[2,1,32,2,512]{4,2,1,3,0:T(8,128)(2,1)S(1)}, u32[]{:S(2)}, u32[]{:S(2)}) collective-permute-start(bf16[2,1,32,2,512]{4,2,1,3,0:T(8,128)(2,1)S(1)} %get-tuple-element.21), channel_id=1, source_target_pairs={{0,1},{1,0},{2,3},{3,2},{4,5},{5,4},{6,7},{7,6},{8,9},{9,8},{10,11... | collective-permute-start | bytes 393224 | tf_op jit(solution)/shard_map/ppermute | solution.py:18
  162.3 7.8 %collective-permute-start.16 = (bf16[2,1,32,2,512]{4,2,1,3,0:T(8,128)(2,1)S(1)}, bf16[2,1,32,2,512]{4,2,1,3,0:T(8,128)(2,1)S(1)}, u32[]{:S(2)}, u32[]{:S(2)}) collective-permute-start(bf16[2,1,32,2,512]{4,2,1,3,0:T(8,128)(2,1)S(1)} %get-tuple-element.20), channel_id=1, source_target_pairs={{0,2},{1,3},{2,0},{3,1},{4,6},{5,7},{6,4},{7,5},{8,10},{9,11},{10,... | collective-permute-start | bytes 393224 | tf_op jit(solution)/shard_map/ppermute | solution.py:18
  162.6 9.1 %collective-permute-start.17 = (bf16[2,1,32,2,512]{4,2,1,3,0:T(8,128)(2,1)S(1)}, bf16[2,1,32,2,512]{4,2,1,3,0:T(8,128)(2,1)S(1)}, u32[]{:S(2)}, u32[]{:S(2)}) collective-permute-start(bf16[2,1,32,2,512]{4,2,1,3,0:T(8,128)(2,1)S(1)} %get-tuple-element.19), channel_id=1, source_target_pairs={{0,3},{1,2},{2,1},{3,0},{4,7},{5,6},{6,5},{7,4},{8,11},{9,10},{10,... | collective-permute-start | bytes 393224 | tf_op jit(solution)/shard_map/ppermute | solution.py:18
  164.0 9.2 %collective-permute-start.18 = (bf16[2,1,32,2,512]{4,2,1,3,0:T(8,128)(2,1)S(1)}, bf16[2,1,32,2,512]{4,2,1,3,0:T(8,128)(2,1)S(1)}, u32[]{:S(2)}, u32[]{:S(2)}) collective-permute-start(bf16[2,1,32,2,512]{4,2,1,3,0:T(8,128)(2,1)S(1)} %get-tuple-element.18), channel_id=1, source_target_pairs={{0,4},{1,5},{2,6},{3,7},{4,0},{5,1},{6,2},{7,3},{8,12},{9,13},{10,... | collective-permute-start | bytes 393224 | tf_op jit(solution)/shard_map/ppermute | solution.py:18
  165.2 9.3 %collective-permute-start.19 = (bf16[2,1,32,2,512]{4,2,1,3,0:T(8,128)(2,1)S(1)}, bf16[2,1,32,2,512]{4,2,1,3,0:T(8,128)(2,1)S(1)}, u32[]{:S(2)}, u32[]{:S(2)}) collective-permute-start(bf16[2,1,32,2,512]{4,2,1,3,0:T(8,128)(2,1)S(1)} %get-tuple-element.17), channel_id=1, source_target_pairs={{0,5},{1,4},{2,7},{3,6},{4,1},{5,0},{6,3},{7,2},{8,13},{9,12},{10,... | collective-permute-start | bytes 393224 | tf_op jit(solution)/shard_map/ppermute | solution.py:18
  168.9 42.0 %copy-start.7 = (bf16[1,512,2,512]{3,1,2,0:T(8,128)(2,1)S(1)}, bf16[1,512,2,512]{3,1,2,0:T(8,128)(2,1)}, u32[]{:S(2)}) copy-start(bf16[1,512,2,512]{3,1,2,0:T(8,128)(2,1)} %get-tuple-element.51) | copy-start | bytes 3145732
  168.9 7.2 %collective-permute-start.20 = (bf16[2,1,32,2,512]{4,2,1,3,0:T(8,128)(2,1)S(1)}, bf16[2,1,32,2,512]{4,2,1,3,0:T(8,128)(2,1)S(1)}, u32[]{:S(2)}, u32[]{:S(2)}) collective-permute-start(bf16[2,1,32,2,512]{4,2,1,3,0:T(8,128)(2,1)S(1)} %get-tuple-element.16), channel_id=1, source_target_pairs={{0,6},{1,7},{2,4},{3,5},{4,2},{5,3},{6,0},{7,1},{8,14},{9,15},{10,... | collective-permute-start | bytes 393224 | tf_op jit(solution)/shard_map/ppermute | solution.py:18
  170.1 12.2 %collective-permute-start.21 = (bf16[2,1,32,2,512]{4,2,1,3,0:T(8,128)(2,1)S(1)}, bf16[2,1,32,2,512]{4,2,1,3,0:T(8,128)(2,1)S(1)}, u32[]{:S(2)}, u32[]{:S(2)}) collective-permute-start(bf16[2,1,32,2,512]{4,2,1,3,0:T(8,128)(2,1)S(1)} %get-tuple-element.15), channel_id=1, source_target_pairs={{0,7},{1,6},{2,5},{3,4},{4,3},{5,2},{6,1},{7,0},{8,15},{9,14},{10,... | collective-permute-start | bytes 393224 | tf_op jit(solution)/shard_map/ppermute | solution.py:18
  171.7 12.4 %collective-permute-start.22 = (bf16[2,1,32,2,512]{4,2,1,3,0:T(8,128)(2,1)S(1)}, bf16[2,1,32,2,512]{4,2,1,3,0:T(8,128)(2,1)S(1)}, u32[]{:S(2)}, u32[]{:S(2)}) collective-permute-start(bf16[2,1,32,2,512]{4,2,1,3,0:T(8,128)(2,1)S(1)} %get-tuple-element.14), channel_id=1, source_target_pairs={{0,8},{1,9},{2,10},{3,11},{4,12},{5,13},{6,14},{7,15},{8,0},{9,1},... | collective-permute-start | bytes 393224 | tf_op jit(solution)/shard_map/ppermute | solution.py:18
  173.3 25.2 %collective-permute-start.23 = (bf16[2,1,32,2,512]{4,2,1,3,0:T(8,128)(2,1)S(1)}, bf16[2,1,32,2,512]{4,2,1,3,0:T(8,128)(2,1)S(1)}, u32[]{:S(2)}, u32[]{:S(2)}) collective-permute-start(bf16[2,1,32,2,512]{4,2,1,3,0:T(8,128)(2,1)S(1)} %get-tuple-element.13), channel_id=1, source_target_pairs={{0,9},{1,8},{2,11},{3,10},{4,13},{5,12},{6,15},{7,14},{8,1},{9,0},... | collective-permute-start | bytes 393224 | tf_op jit(solution)/shard_map/ppermute | solution.py:18
  174.5 25.5 %collective-permute-start.24 = (bf16[2,1,32,2,512]{4,2,1,3,0:T(8,128)(2,1)S(1)}, bf16[2,1,32,2,512]{4,2,1,3,0:T(8,128)(2,1)S(1)}, u32[]{:S(2)}, u32[]{:S(2)}) collective-permute-start(bf16[2,1,32,2,512]{4,2,1,3,0:T(8,128)(2,1)S(1)} %get-tuple-element.12), channel_id=1, source_target_pairs={{0,10},{1,11},{2,8},{3,9},{4,14},{5,15},{6,12},{7,13},{8,2},{9,3},... | collective-permute-start | bytes 393224 | tf_op jit(solution)/shard_map/ppermute | solution.py:18
  176.1 33.3 %collective-permute-start.25 = (bf16[2,1,32,2,512]{4,2,1,3,0:T(8,128)(2,1)S(1)}, bf16[2,1,32,2,512]{4,2,1,3,0:T(8,128)(2,1)S(1)}, u32[]{:S(2)}, u32[]{:S(2)}) collective-permute-start(bf16[2,1,32,2,512]{4,2,1,3,0:T(8,128)(2,1)S(1)} %get-tuple-element.11), channel_id=1, source_target_pairs={{0,11},{1,10},{2,9},{3,8},{4,15},{5,14},{6,13},{7,12},{8,3},{9,2},... | collective-permute-start | bytes 393224 | tf_op jit(solution)/shard_map/ppermute | solution.py:18
  182.3 27.1 %collective-permute-start.26 = (bf16[2,1,32,2,512]{4,2,1,3,0:T(8,128)(2,1)S(1)}, bf16[2,1,32,2,512]{4,2,1,3,0:T(8,128)(2,1)S(1)}, u32[]{:S(2)}, u32[]{:S(2)}) collective-permute-start(bf16[2,1,32,2,512]{4,2,1,3,0:T(8,128)(2,1)S(1)} %get-tuple-element.10), channel_id=1, source_target_pairs={{0,12},{1,13},{2,14},{3,15},{4,8},{5,9},{6,10},{7,11},{8,4},{9,5},... | collective-permute-start | bytes 393224 | tf_op jit(solution)/shard_map/ppermute | solution.py:18
  184.0 25.4 %collective-permute-start.27 = (bf16[2,1,32,2,512]{4,2,1,3,0:T(8,128)(2,1)S(1)}, bf16[2,1,32,2,512]{4,2,1,3,0:T(8,128)(2,1)S(1)}, u32[]{:S(2)}, u32[]{:S(2)}) collective-permute-start(bf16[2,1,32,2,512]{4,2,1,3,0:T(8,128)(2,1)S(1)} %get-tuple-element.9), channel_id=1, source_target_pairs={{0,13},{1,12},{2,15},{3,14},{4,9},{5,8},{6,11},{7,10},{8,5},{9,4},... | collective-permute-start | bytes 393224 | tf_op jit(solution)/shard_map/ppermute | solution.py:18
  198.4 11.0 %collective-permute-start.28 = (bf16[2,1,32,2,512]{4,2,1,3,0:T(8,128)(2,1)S(1)}, bf16[2,1,32,2,512]{4,2,1,3,0:T(8,128)(2,1)S(1)}, u32[]{:S(2)}, u32[]{:S(2)}) collective-permute-start(bf16[2,1,32,2,512]{4,2,1,3,0:T(8,128)(2,1)S(1)} %get-tuple-element.8), channel_id=1, source_target_pairs={{0,14},{1,15},{2,12},{3,13},{4,10},{5,11},{6,8},{7,9},{8,6},{9,7},... | collective-permute-start | bytes 393224 | tf_op jit(solution)/shard_map/ppermute | solution.py:18
  200.0 9.5 %collective-permute-start.29 = (bf16[2,1,32,2,512]{4,2,1,3,0:T(8,128)(2,1)S(1)}, bf16[2,1,32,2,512]{4,2,1,3,0:T(8,128)(2,1)S(1)}, u32[]{:S(2)}, u32[]{:S(2)}) collective-permute-start(bf16[2,1,32,2,512]{4,2,1,3,0:T(8,128)(2,1)S(1)} %get-tuple-element.7), channel_id=1, source_target_pairs={{0,15},{1,14},{2,13},{3,12},{4,11},{5,10},{6,9},{7,8},{8,7},{9,6},... | collective-permute-start | bytes 393224 | tf_op jit(solution)/shard_map/ppermute | solution.py:18
  209.5 1.4 copy-start.1
Sparse Core Ops, SparseCore 0:
  9.5 81.2 all-gather.2
  93.0 52.9 all-gather.4
